TPU v7x, 32 devices: a whole 2x2x4 slice. The times are simulated.
32 devices in a mesh: gx: 4 (over z), gy: 4 (over y, core), gz: 2 (over x).
Axes of the slice: x: 2, y: 2, z: 4, core: 2. Of those that a mesh axis runs over, the one named last changes fastest.
Arguments:
- volume: bfloat16 [32, 64, 32, 128], P('gx', 'gy', 'gz'), may hold values from -6 to 6
- w_full: bfloat16 [3, 3, 3, 128, 128], replicated, may hold values from -0.15625 to 0.15625
- w_half: bfloat16 [3, 3, 3, 128, 256], replicated, may hold values from -0.15625 to 0.15625
- w_bottom_in: bfloat16 [3, 3, 3, 256, 512], P(None, None, None, None, 'gx'), may hold values from -0.109375 to 0.109375
- w_bottom_out: bfloat16 [3, 3, 3, 512, 512], P(None, None, None, None, 'gx'), may hold values from -0.078125 to 0.078125
- w_up: bfloat16 [3, 3, 3, 768, 256], replicated, may hold values from -0.0625 to 0.0625
Outputs:
- decoded: bfloat16 [16, 32, 16, 256], P('gx', 'gy', 'gz')
All inputs are finite; a program needn't handle non-finite values.
Results may differ from a plain program's by a relative error of at most 0.009.
Values may be sent and summed in bfloat16 or wider, within the bound.
A program may use at most 64 MiB of HBM per device.

v0:
```python
import jax
import jax.numpy as jnp
from jax import lax
from jax.sharding import PartitionSpec as P


def with_halo(cells, sides, width):
    for axis, dim in sides:
        count = lax.axis_size(axis)
        ends = count - 1
        head = lax.slice_in_dim(cells, 0, width, axis=dim)
        tail = lax.slice_in_dim(cells, cells.shape[dim] - width, cells.shape[dim], axis=dim)
        cells = jnp.concatenate(
            [
                lax.ppermute(tail, axis, [(i, (i + 1) % count) for i in range(ends)]),
                cells,
                lax.ppermute(head, axis, [((i + 1) % count, i) for i in range(ends)]),
            ],
            axis=dim,
        )
    return cells


def convolve(padded, kernel):
    size_x = padded.shape[0] - 2
    size_y = padded.shape[1] - 2
    size_z = padded.shape[2] - 2
    channels = padded.shape[3]
    total = jnp.zeros((size_x * size_y * size_z, kernel.shape[4]), jnp.float32)
    for offset_x in range(3):
        for offset_y in range(3):
            for offset_z in range(3):
                window = padded[
                    offset_x : offset_x + size_x,
                    offset_y : offset_y + size_y,
                    offset_z : offset_z + size_z,
                    :,
                ]
                total = total + jnp.dot(
                    window.reshape(-1, channels),
                    kernel[offset_x, offset_y, offset_z],
                    preferred_element_type=jnp.float32,
                )
    return total.reshape(size_x, size_y, size_z, kernel.shape[4])


def rectify(total):
    return jnp.maximum(total, 0.0).astype(jnp.bfloat16)


def shrink(field):
    size_x, size_y, size_z, channels = field.shape
    blocks = field.reshape(size_x // 2, 2, size_y // 2, 2, size_z // 2, 2, channels)
    return jnp.max(blocks, axis=(1, 3, 5))


def enlarge(field):
    size_x, size_y, size_z, channels = field.shape
    spread = jnp.broadcast_to(
        field[:, None, :, None, :, None, :], (size_x, 2, size_y, 2, size_z, 2, channels)
    )
    return spread.reshape(2 * size_x, 2 * size_y, 2 * size_z, channels)


def pad_first(field):
    return jnp.pad(field, ((1, 1), (0, 0), (0, 0), (0, 0)))


def on_device(volume, w_full, w_half, w_bottom_in, w_bottom_out, w_up):
    padded = with_halo(volume, (("gx", 0), ("gy", 1), ("gz", 2)), 1)
    full_level = rectify(convolve(padded, w_full))
    pooled = shrink(full_level)
    pooled_rim = with_halo(pooled, (("gx", 0), ("gy", 1), ("gz", 2)), 1)
    skip_level = rectify(convolve(pooled_rim, w_half))
    coarse = shrink(skip_level)
    column = lax.all_gather(coarse, "gx", axis=0, tiled=True)
    column = with_halo(column, (("gy", 1), ("gz", 2)), 1)
    bottom_first = rectify(convolve(pad_first(column), w_bottom_in))
    filters = lax.all_gather(bottom_first, "gx", axis=3, tiled=True)
    filters = with_halo(filters, (("gy", 1), ("gz", 2)), 1)
    bottom_second = rectify(convolve(pad_first(filters), w_bottom_out))
    regrouped = lax.all_to_all(bottom_second, "gx", split_axis=0, concat_axis=3, tiled=True)
    joined = jnp.concatenate([enlarge(regrouped), skip_level], axis=3)
    joined = with_halo(joined, (("gx", 0), ("gy", 1), ("gz", 2)), 1)
    return convolve(joined, w_up).astype(jnp.bfloat16)


def solution(mesh):
    return jax.shard_map(
        on_device,
        mesh=mesh,
        in_specs=(
            P("gx", "gy", "gz", None),
            P(),
            P(),
            P(None, None, None, None, "gx"),
            P(None, None, None, None, "gx"),
            P(),
        ),
        out_specs=P("gx", "gy", "gz", None),
        check_vma=False,
    )
```

profile of v0, /device:TPU:1, one launch (start us, length us, event | category | flops | bytes accessed | tf_op | source)
XLA Modules:
  0.0 225.6 jit_solution(15556953054492281344)
XLA Ops:
  0.9 4.0 %collective-permute-start = (bf16[1,16,16,128]{3,2,1,0:T(8,128)(2,1)S(1)}, bf16[1,16,16,128]{3,2,1,0:T(8,128)(2,1)S(1)}, u32[]{:S(2)}, u32[]{:S(2)}) collective-permute-start(bf16[1,16,16,128]{3,2,1,0:T(8,128)(2,1)S(1)} %get-tuple-element.74), channel_id=1, source_target_pairs={{0,8},{8,16},{16,24},{1,9},{9,17},{17,25},{2,10},{10,18},{18,26},{... | collective-permute-start | bytes 196616 | tf_op jit(solution)/shard_map/ppermute | solution.py:15
  6.2 3.7 %collective-permute-done.1 = bf16[1,16,16,128]{3,2,1,0:T(8,128)(2,1)S(1)} collective-permute-done((bf16[1,16,16,128]{3,2,1,0:T(8,128)(2,1)S(1)}, bf16[1,16,16,128]{3,2,1,0:T(8,128)(2,1)S(1)}, u32[]{:S(2)}, u32[]{:S(2)}) %collective-permute-start.1) | collective-permute-done | bytes 65568 | tf_op jit(solution)/shard_map/ppermute | solution.py:17
  9.9 1.8 pad_maximum_fusion.4
  11.8 5.1 %collective-permute-start.2 = (bf16[10,1,16,128]{3,2,1,0:T(8,128)(2,1)S(1)}, bf16[10,1,16,128]{3,2,1,0:T(8,128)(2,1)S(1)}, u32[]{:S(2)}, u32[]{:S(2)}) collective-permute-start(bf16[10,1,16,128]{3,2,1,0:T(8,128)(2,1)S(1)} %get-tuple-element.64), channel_id=1, source_target_pairs={{0,2},{2,4},{4,6},{1,3},{3,5},{5,7},{8,10},{10,12},{12,14},{9,11},... | collective-permute-start | bytes 122888 | tf_op jit(solution)/shard_map/ppermute | solution.py:15
  16.9 1.9 collective-permute-start.3
  18.9 3.4 %collective-permute-done.3 = bf16[10,1,16,128]{3,2,1,0:T(8,128)(2,1)S(1)} collective-permute-done((bf16[10,1,16,128]{3,2,1,0:T(8,128)(2,1)S(1)}, bf16[10,1,16,128]{3,2,1,0:T(8,128)(2,1)S(1)}, u32[]{:S(2)}, u32[]{:S(2)}) %collective-permute-start.3) | collective-permute-done | bytes 40992 | tf_op jit(solution)/shard_map/ppermute | solution.py:17
  22.4 3.1 %collective-permute-start.4 = (bf16[10,18,1,128]{3,2,1,0:T(2,128)(2,1)S(1)}, bf16[10,18,1,128]{3,2,1,0:T(2,128)(2,1)S(1)}, u32[]{:S(2)}, u32[]{:S(2)}) collective-permute-start(bf16[10,18,1,128]{3,2,1,0:T(2,128)(2,1)S(1)} %get-tuple-element.47), channel_id=1, source_target_pairs={{0,1},{2,3},{4,5},{6,7},{8,9},{10,11},{12,13},{14,15},{16,17},{18,... | collective-permute-start | bytes 138248 | tf_op jit(solution)/shard_map/ppermute | solution.py:15
  27.5 3.5 %collective-permute-done.5 = bf16[10,18,1,128]{3,2,1,0:T(2,128)(2,1)S(1)} collective-permute-done((bf16[10,18,1,128]{3,2,1,0:T(2,128)(2,1)S(1)}, bf16[10,18,1,128]{3,2,1,0:T(2,128)(2,1)S(1)}, u32[]{:S(2)}, u32[]{:S(2)}) %collective-permute-start.5) | collective-permute-done | bytes 46112 | tf_op jit(solution)/shard_map/ppermute | solution.py:17
  31.8 2.6 %fusion.380 = (bf16[8,16,16,128]{3,2,1,0:T(8,128)(2,1)S(1)}, bf16[8,16,16,128]{3,2,1,0:T(8,128)(2,1)S(1)}, bf16[8,16,16,128]{3,2,1,0:T(8,128)(2,1)S(1)}, bf16[8,...) fusion(bf16[10,18,17,128]{3,2,1,0:T(8,128)(2,1)S(1)} %get-tuple, ...), kind=kLoop, calls=%fused_computation.565 | loop fusion | bytes 18874368 | tf_op jit(solution)/shard_map/slice | solution.py:33
  43.4 3.2 %collective-permute-start.6 = (bf16[1,8,8,128]{3,2,1,0:T(8,128)(2,1)S(1)}, bf16[1,8,8,128]{3,2,1,0:T(8,128)(2,1)S(1)}, u32[]{:S(2)}, u32[]{:S(2)}) collective-permute-start(bf16[1,8,8,128]{3,2,1,0:T(8,128)(2,1)S(1)} %get-tuple-element.181), channel_id=1, source_target_pairs={{0,8},{8,16},{16,24},{1,9},{9,17},{17,25},{2,10},{10,18},{18,26},{... | collective-permute-start | bytes 49160 | tf_op jit(solution)/shard_map/ppermute | solution.py:15
  47.9 3.6 %collective-permute-done.7 = bf16[1,8,8,128]{3,2,1,0:T(8,128)(2,1)S(1)} collective-permute-done((bf16[1,8,8,128]{3,2,1,0:T(8,128)(2,1)S(1)}, bf16[1,8,8,128]{3,2,1,0:T(8,128)(2,1)S(1)}, u32[]{:S(2)}, u32[]{:S(2)}) %collective-permute-start.7) | collective-permute-done | bytes 16416 | tf_op jit(solution)/shard_map/ppermute | solution.py:17
  51.5 4.3 %collective-permute-start.8 = (bf16[6,1,8,128]{3,2,1,0:T(8,128)(2,1)S(1)}, bf16[6,1,8,128]{3,2,1,0:T(8,128)(2,1)S(1)}, u32[]{:S(2)}, u32[]{:S(2)}) collective-permute-start(bf16[6,1,8,128]{3,2,1,0:T(8,128)(2,1)S(1)} %get-tuple-element.172), channel_id=1, source_target_pairs={{0,2},{2,4},{4,6},{1,3},{3,5},{5,7},{8,10},{10,12},{12,14},{9,11},... | collective-permute-start | bytes 36872 | tf_op jit(solution)/shard_map/ppermute | solution.py:15
  55.8 1.9 collective-permute-start.9
  57.8 3.1 %collective-permute-done.9 = bf16[6,1,8,128]{3,2,1,0:T(8,128)(2,1)S(1)} collective-permute-done((bf16[6,1,8,128]{3,2,1,0:T(8,128)(2,1)S(1)}, bf16[6,1,8,128]{3,2,1,0:T(8,128)(2,1)S(1)}, u32[]{:S(2)}, u32[]{:S(2)}) %collective-permute-start.9) | collective-permute-done | bytes 12320 | tf_op jit(solution)/shard_map/ppermute | solution.py:17
  63.8 3.1 %collective-permute-done.11 = bf16[6,10,1,128]{3,2,1,0:T(2,128)(2,1)S(1)} collective-permute-done((bf16[6,10,1,128]{3,2,1,0:T(2,128)(2,1)S(1)}, bf16[6,10,1,128]{3,2,1,0:T(2,128)(2,1)S(1)}, u32[]{:S(2)}, u32[]{:S(2)}) %collective-permute-start.11) | collective-permute-done | bytes 15392 | tf_op jit(solution)/shard_map/ppermute | solution.py:17
  72.1 10.6 %all_gather.6 = bf16[8,4,4,256]{3,2,1,0:T(4,128)(2,1)S(1)} all-gather(bf16[2,4,4,256]{3,2,1,0:T(4,128)(2,1)S(1)} %reduce_max.19), channel_id=1, replica_groups=mesh['gx'=4,'gy'=4,'gz'=2] {'gx'}, dimensions={0}, use_global_device_ids=true | all-gather | bytes 81920 | tf_op jit(solution)/shard_map/all_gather | solution.py:76
  82.7 5.9 %collective-permute-start.12 = (bf16[8,1,4,256]{3,2,1,0:T(4,128)(2,1)S(1)}, bf16[8,1,4,256]{3,2,1,0:T(4,128)(2,1)S(1)}, u32[]{:S(2)}, u32[]{:S(2)}) collective-permute-start(bf16[8,1,4,256]{3,2,1,0:T(4,128)(2,1)S(1)} %get-tuple-element.178), channel_id=1, source_target_pairs={{0,2},{2,4},{4,6},{1,3},{3,5},{5,7},{8,10},{10,12},{12,14},{9,11},... | collective-permute-start | bytes 49160 | tf_op jit(solution)/shard_map/ppermute | solution.py:15
  88.6 2.1 collective-permute-start.13
  90.8 3.1 %collective-permute-done.13 = bf16[8,1,4,256]{3,2,1,0:T(4,128)(2,1)S(1)} collective-permute-done((bf16[8,1,4,256]{3,2,1,0:T(4,128)(2,1)S(1)}, bf16[8,1,4,256]{3,2,1,0:T(4,128)(2,1)S(1)}, u32[]{:S(2)}, u32[]{:S(2)}) %collective-permute-start.13) | collective-permute-done | bytes 16416 | tf_op jit(solution)/shard_map/ppermute | solution.py:17
  97.9 2.5 %collective-permute-done.15 = bf16[8,6,1,256]{3,2,1,0:T(2,128)(2,1)S(1)} collective-permute-done((bf16[8,6,1,256]{3,2,1,0:T(2,128)(2,1)S(1)}, bf16[8,6,1,256]{3,2,1,0:T(2,128)(2,1)S(1)}, u32[]{:S(2)}, u32[]{:S(2)}) %collective-permute-start.15) | collective-permute-done | bytes 24608 | tf_op jit(solution)/shard_map/ppermute | solution.py:17
  114.9 9.0 %all_gather.7 = bf16[8,4,4,512]{3,2,1,0:T(4,128)(2,1)S(1)} all-gather(bf16[8,4,4,128]{3,2,1,0:T(4,128)(2,1)S(1)} %bitcast.716), channel_id=1, replica_groups=mesh['gx'=4,'gy'=4,'gz'=2] {'gx'}, dimensions={3}, use_global_device_ids=true | all-gather | bytes 163840 | tf_op jit(solution)/shard_map/all_gather | solution.py:79
  123.9 4.6 %collective-permute-start.16 = (bf16[8,1,4,512]{3,2,1,0:T(4,128)(2,1)S(1)}, bf16[8,1,4,512]{3,2,1,0:T(4,128)(2,1)S(1)}, u32[]{:S(2)}, u32[]{:S(2)}) collective-permute-start(bf16[8,1,4,512]{3,2,1,0:T(4,128)(2,1)S(1)} %get-tuple-element.154), channel_id=1, source_target_pairs={{0,2},{2,4},{4,6},{1,3},{3,5},{5,7},{8,10},{10,12},{12,14},{9,11},... | collective-permute-start | bytes 98312 | tf_op jit(solution)/shard_map/ppermute | solution.py:15
  128.5 1.9 collective-permute-start.17
  130.5 3.3 %collective-permute-done.17 = bf16[8,1,4,512]{3,2,1,0:T(4,128)(2,1)S(1)} collective-permute-done((bf16[8,1,4,512]{3,2,1,0:T(4,128)(2,1)S(1)}, bf16[8,1,4,512]{3,2,1,0:T(4,128)(2,1)S(1)}, u32[]{:S(2)}, u32[]{:S(2)}) %collective-permute-start.17) | collective-permute-done | bytes 32800 | tf_op jit(solution)/shard_map/ppermute | solution.py:17
  138.6 2.3 %collective-permute-done.19 = bf16[8,6,1,512]{3,2,1,0:T(2,128)(2,1)S(1)} collective-permute-done((bf16[8,6,1,512]{3,2,1,0:T(2,128)(2,1)S(1)}, bf16[8,6,1,512]{3,2,1,0:T(2,128)(2,1)S(1)}, u32[]{:S(2)}, u32[]{:S(2)}) %collective-permute-start.19) | collective-permute-done | bytes 49184 | tf_op jit(solution)/shard_map/ppermute | solution.py:17
  145.1 2.6 %pad_maximum_fusion.20 = (bf16[8,4,4,512]{3,2,1,0:T(4,128)(2,1)S(1)}, bf16[8,4,4,512]{3,2,1,0:T(4,128)(2,1)}, bf16[8,4,4,512]{3,2,1,0:T(4,128)(2,1)S(1)}, bf16[8...) fusion(bf16[8,6,4,512]{3,2,1,0:T(4,128)(2,1)S(1)} %constant_dynamic-update-slice, ...), kind=kLoop, calls=%fused_computation.288 | loop fusion | flops 1572864 | bytes 1081344 | tf_op jit(solution)/shard_map/concatenate | solution.py:13
  178.0 6.9 %all_to_all.15 = bf16[8,4,4,128]{3,2,1,0:T(4,128)(2,1)S(1)} all-to-all(bf16[8,4,4,128]{3,2,1,0:T(4,128)(2,1)S(1)} %bitcast.718), channel_id=1, replica_groups=mesh['gx'=4,'gy'=4,'gz'=2] {'gx'}, dimensions={0} | all-to-all | bytes 65536 | tf_op jit(solution)/shard_map/all_to_all | solution.py:82
  185.4 2.4 %collective-permute-start.20 = (bf16[1,8,8,768]{3,2,1,0:T(8,128)(2,1)S(1)}, bf16[1,8,8,768]{3,2,1,0:T(8,128)(2,1)S(1)}, u32[]{:S(2)}, u32[]{:S(2)}) collective-permute-start(bf16[1,8,8,768]{3,2,1,0:T(8,128)(2,1)S(1)} %get-tuple-element.95), channel_id=1, source_target_pairs={{0,8},{8,16},{16,24},{1,9},{9,17},{17,25},{2,10},{10,18},{18,26},{... | collective-permute-start | bytes 294920 | tf_op jit(solution)/shard_map/ppermute | solution.py:15
  190.4 2.8 %collective-permute-done.21 = bf16[1,8,8,768]{3,2,1,0:T(8,128)(2,1)S(1)} collective-permute-done((bf16[1,8,8,768]{3,2,1,0:T(8,128)(2,1)S(1)}, bf16[1,8,8,768]{3,2,1,0:T(8,128)(2,1)S(1)}, u32[]{:S(2)}, u32[]{:S(2)}) %collective-permute-start.21) | collective-permute-done | bytes 98336 | tf_op jit(solution)/shard_map/ppermute | solution.py:17
  194.5 5.8 %collective-permute-start.22 = (bf16[6,1,8,768]{3,2,1,0:T(8,128)(2,1)S(1)}, bf16[6,1,8,768]{3,2,1,0:T(8,128)(2,1)S(1)}, u32[]{:S(2)}, u32[]{:S(2)}) collective-permute-start(bf16[6,1,8,768]{3,2,1,0:T(8,128)(2,1)S(1)} %get-tuple-element.68), channel_id=1, source_target_pairs={{0,2},{2,4},{4,6},{1,3},{3,5},{5,7},{8,10},{10,12},{12,14},{9,11},... | collective-permute-start | bytes 221192 | tf_op jit(solution)/shard_map/ppermute | solution.py:15
  200.4 1.9 collective-permute-start.23
  203.6 2.5 %collective-permute-done.23 = bf16[6,1,8,768]{3,2,1,0:T(8,128)(2,1)S(1)} collective-permute-done((bf16[6,1,8,768]{3,2,1,0:T(8,128)(2,1)S(1)}, bf16[6,1,8,768]{3,2,1,0:T(8,128)(2,1)S(1)}, u32[]{:S(2)}, u32[]{:S(2)}) %collective-permute-start.23) | collective-permute-done | bytes 73760 | tf_op jit(solution)/shard_map/ppermute | solution.py:17
  (295 shorter events, 105.3 us)
Async XLA Ops:
  0.9 5.3 %collective-permute-start = (bf16[1,16,16,128]{3,2,1,0:T(8,128)(2,1)S(1)}, bf16[1,16,16,128]{3,2,1,0:T(8,128)(2,1)S(1)}, u32[]{:S(2)}, u32[]{:S(2)}) collective-permute-start(bf16[1,16,16,128]{3,2,1,0:T(8,128)(2,1)S(1)} %get-tuple-element.74), channel_id=1, source_target_pairs={{0,8},{8,16},{16,24},{1,9},{9,17},{17,25},{2,10},{10,18},{18,26},{... | collective-permute-start | bytes 196616 | tf_op jit(solution)/shard_map/ppermute | solution.py:15
  4.9 5.0 %collective-permute-start.1 = (bf16[1,16,16,128]{3,2,1,0:T(8,128)(2,1)S(1)}, bf16[1,16,16,128]{3,2,1,0:T(8,128)(2,1)S(1)}, u32[]{:S(2)}, u32[]{:S(2)}) collective-permute-start(bf16[1,16,16,128]{3,2,1,0:T(8,128)(2,1)S(1)} %get-tuple-element.73), channel_id=1, source_target_pairs={{8,0},{16,8},{24,16},{9,1},{17,9},{25,17},{10,2},{18,10},{26,18},{... | collective-permute-start | bytes 196616 | tf_op jit(solution)/shard_map/ppermute | solution.py:17
  11.8 7.1 %collective-permute-start.2 = (bf16[10,1,16,128]{3,2,1,0:T(8,128)(2,1)S(1)}, bf16[10,1,16,128]{3,2,1,0:T(8,128)(2,1)S(1)}, u32[]{:S(2)}, u32[]{:S(2)}) collective-permute-start(bf16[10,1,16,128]{3,2,1,0:T(8,128)(2,1)S(1)} %get-tuple-element.64), channel_id=1, source_target_pairs={{0,2},{2,4},{4,6},{1,3},{3,5},{5,7},{8,10},{10,12},{12,14},{9,11},... | collective-permute-start | bytes 122888 | tf_op jit(solution)/shard_map/ppermute | solution.py:15
  16.9 5.3 %collective-permute-start.3 = (bf16[10,1,16,128]{3,2,1,0:T(8,128)(2,1)S(1)}, bf16[10,1,16,128]{3,2,1,0:T(8,128)(2,1)S(1)}, u32[]{:S(2)}, u32[]{:S(2)}) collective-permute-start(bf16[10,1,16,128]{3,2,1,0:T(8,128)(2,1)S(1)} %get-tuple-element.65), channel_id=1, source_target_pairs={{2,0},{4,2},{6,4},{3,1},{5,3},{7,5},{10,8},{12,10},{14,12},{11,9},... | collective-permute-start | bytes 122888 | tf_op jit(solution)/shard_map/ppermute | solution.py:17
  22.4 5.1 %collective-permute-start.4 = (bf16[10,18,1,128]{3,2,1,0:T(2,128)(2,1)S(1)}, bf16[10,18,1,128]{3,2,1,0:T(2,128)(2,1)S(1)}, u32[]{:S(2)}, u32[]{:S(2)}) collective-permute-start(bf16[10,18,1,128]{3,2,1,0:T(2,128)(2,1)S(1)} %get-tuple-element.47), channel_id=1, source_target_pairs={{0,1},{2,3},{4,5},{6,7},{8,9},{10,11},{12,13},{14,15},{16,17},{18,... | collective-permute-start | bytes 138248 | tf_op jit(solution)/shard_map/ppermute | solution.py:15
  25.5 5.4 %collective-permute-start.5 = (bf16[10,18,1,128]{3,2,1,0:T(2,128)(2,1)S(1)}, bf16[10,18,1,128]{3,2,1,0:T(2,128)(2,1)S(1)}, u32[]{:S(2)}, u32[]{:S(2)}) collective-permute-start(bf16[10,18,1,128]{3,2,1,0:T(2,128)(2,1)S(1)} %get-tuple-element.48), channel_id=1, source_target_pairs={{1,0},{3,2},{5,4},{7,6},{9,8},{11,10},{13,12},{15,14},{17,16},{19,... | collective-permute-start | bytes 138248 | tf_op jit(solution)/shard_map/ppermute | solution.py:17
  42.4 21.2 %copy-start.1 = (bf16[3,3,3,128,256]{4,3,2,1,0:T(8,128)(2,1)S(1)}, bf16[3,3,3,128,256]{4,3,2,1,0:T(8,128)(2,1)}, u32[]{:S(2)}) copy-start(bf16[3,3,3,128,256]{4,3,2,1,0:T(8,128)(2,1)} %param.8) | copy-start | bytes 5308420
  43.4 4.5 %collective-permute-start.6 = (bf16[1,8,8,128]{3,2,1,0:T(8,128)(2,1)S(1)}, bf16[1,8,8,128]{3,2,1,0:T(8,128)(2,1)S(1)}, u32[]{:S(2)}, u32[]{:S(2)}) collective-permute-start(bf16[1,8,8,128]{3,2,1,0:T(8,128)(2,1)S(1)} %get-tuple-element.181), channel_id=1, source_target_pairs={{0,8},{8,16},{16,24},{1,9},{9,17},{17,25},{2,10},{10,18},{18,26},{... | collective-permute-start | bytes 49160 | tf_op jit(solution)/shard_map/ppermute | solution.py:15
  46.6 4.9 %collective-permute-start.7 = (bf16[1,8,8,128]{3,2,1,0:T(8,128)(2,1)S(1)}, bf16[1,8,8,128]{3,2,1,0:T(8,128)(2,1)S(1)}, u32[]{:S(2)}, u32[]{:S(2)}) collective-permute-start(bf16[1,8,8,128]{3,2,1,0:T(8,128)(2,1)S(1)} %get-tuple-element.182), channel_id=1, source_target_pairs={{8,0},{16,8},{24,16},{9,1},{17,9},{25,17},{10,2},{18,10},{26,18},{... | collective-permute-start | bytes 49160 | tf_op jit(solution)/shard_map/ppermute | solution.py:17
  51.5 6.3 %collective-permute-start.8 = (bf16[6,1,8,128]{3,2,1,0:T(8,128)(2,1)S(1)}, bf16[6,1,8,128]{3,2,1,0:T(8,128)(2,1)S(1)}, u32[]{:S(2)}, u32[]{:S(2)}) collective-permute-start(bf16[6,1,8,128]{3,2,1,0:T(8,128)(2,1)S(1)} %get-tuple-element.172), channel_id=1, source_target_pairs={{0,2},{2,4},{4,6},{1,3},{3,5},{5,7},{8,10},{10,12},{12,14},{9,11},... | collective-permute-start | bytes 36872 | tf_op jit(solution)/shard_map/ppermute | solution.py:15
  55.8 5.0 %collective-permute-start.9 = (bf16[6,1,8,128]{3,2,1,0:T(8,128)(2,1)S(1)}, bf16[6,1,8,128]{3,2,1,0:T(8,128)(2,1)S(1)}, u32[]{:S(2)}, u32[]{:S(2)}) collective-permute-start(bf16[6,1,8,128]{3,2,1,0:T(8,128)(2,1)S(1)} %get-tuple-element.173), channel_id=1, source_target_pairs={{2,0},{4,2},{6,4},{3,1},{5,3},{7,5},{10,8},{12,10},{14,12},{11,9},... | collective-permute-start | bytes 36872 | tf_op jit(solution)/shard_map/ppermute | solution.py:17
  61.0 2.8 %collective-permute-start.10 = (bf16[6,10,1,128]{3,2,1,0:T(2,128)(2,1)S(1)}, bf16[6,10,1,128]{3,2,1,0:T(2,128)(2,1)S(1)}, u32[]{:S(2)}, u32[]{:S(2)}) collective-permute-start(bf16[6,10,1,128]{3,2,1,0:T(2,128)(2,1)S(1)} %get-tuple-element.157), channel_id=1, source_target_pairs={{0,1},{2,3},{4,5},{6,7},{8,9},{10,11},{12,13},{14,15},{16,17},{18,... | collective-permute-start | bytes 46088 | tf_op jit(solution)/shard_map/ppermute | solution.py:15
  62.3 4.6 %collective-permute-start.11 = (bf16[6,10,1,128]{3,2,1,0:T(2,128)(2,1)S(1)}, bf16[6,10,1,128]{3,2,1,0:T(2,128)(2,1)S(1)}, u32[]{:S(2)}, u32[]{:S(2)}) collective-permute-start(bf16[6,10,1,128]{3,2,1,0:T(2,128)(2,1)S(1)} %get-tuple-element.158), channel_id=1, source_target_pairs={{1,0},{3,2},{5,4},{7,6},{9,8},{11,10},{13,12},{15,14},{17,16},{19,... | collective-permute-start | bytes 46088 | tf_op jit(solution)/shard_map/ppermute | solution.py:17
  82.7 8.0 %collective-permute-start.12 = (bf16[8,1,4,256]{3,2,1,0:T(4,128)(2,1)S(1)}, bf16[8,1,4,256]{3,2,1,0:T(4,128)(2,1)S(1)}, u32[]{:S(2)}, u32[]{:S(2)}) collective-permute-start(bf16[8,1,4,256]{3,2,1,0:T(4,128)(2,1)S(1)} %get-tuple-element.178), channel_id=1, source_target_pairs={{0,2},{2,4},{4,6},{1,3},{3,5},{5,7},{8,10},{10,12},{12,14},{9,11},... | collective-permute-start | bytes 49160 | tf_op jit(solution)/shard_map/ppermute | solution.py:15
  88.6 5.2 %collective-permute-start.13 = (bf16[8,1,4,256]{3,2,1,0:T(4,128)(2,1)S(1)}, bf16[8,1,4,256]{3,2,1,0:T(4,128)(2,1)S(1)}, u32[]{:S(2)}, u32[]{:S(2)}) collective-permute-start(bf16[8,1,4,256]{3,2,1,0:T(4,128)(2,1)S(1)} %get-tuple-element.177), channel_id=1, source_target_pairs={{2,0},{4,2},{6,4},{3,1},{5,3},{7,5},{10,8},{12,10},{14,12},{11,9},... | collective-permute-start | bytes 49160 | tf_op jit(solution)/shard_map/ppermute | solution.py:17
  94.0 7.1 %copy-start.2 = (bf16[3,3,3,256,128]{4,3,2,1,0:T(8,128)(2,1)S(1)}, bf16[3,3,3,256,128]{4,3,2,1,0:T(8,128)(2,1)}, u32[]{:S(2)}) copy-start(bf16[3,3,3,256,128]{4,3,2,1,0:T(8,128)(2,1)} %param.9) | copy-start | bytes 5308420
  94.0 3.8 %collective-permute-start.14 = (bf16[8,6,1,256]{3,2,1,0:T(2,128)(2,1)S(1)}, bf16[8,6,1,256]{3,2,1,0:T(2,128)(2,1)S(1)}, u32[]{:S(2)}, u32[]{:S(2)}) collective-permute-start(bf16[8,6,1,256]{3,2,1,0:T(2,128)(2,1)S(1)} %get-tuple-element.168), channel_id=1, source_target_pairs={{0,1},{2,3},{4,5},{6,7},{8,9},{10,11},{12,13},{14,15},{16,17},{18,... | collective-permute-start | bytes 73736 | tf_op jit(solution)/shard_map/ppermute | solution.py:15
  95.5 4.8 %collective-permute-start.15 = (bf16[8,6,1,256]{3,2,1,0:T(2,128)(2,1)S(1)}, bf16[8,6,1,256]{3,2,1,0:T(2,128)(2,1)S(1)}, u32[]{:S(2)}, u32[]{:S(2)}) collective-permute-start(bf16[8,6,1,256]{3,2,1,0:T(2,128)(2,1)S(1)} %get-tuple-element.169), channel_id=1, source_target_pairs={{1,0},{3,2},{5,4},{7,6},{9,8},{11,10},{13,12},{15,14},{17,16},{19,... | collective-permute-start | bytes 73736 | tf_op jit(solution)/shard_map/ppermute | solution.py:17
  123.9 6.5 %collective-permute-start.16 = (bf16[8,1,4,512]{3,2,1,0:T(4,128)(2,1)S(1)}, bf16[8,1,4,512]{3,2,1,0:T(4,128)(2,1)S(1)}, u32[]{:S(2)}, u32[]{:S(2)}) collective-permute-start(bf16[8,1,4,512]{3,2,1,0:T(4,128)(2,1)S(1)} %get-tuple-element.154), channel_id=1, source_target_pairs={{0,2},{2,4},{4,6},{1,3},{3,5},{5,7},{8,10},{10,12},{12,14},{9,11},... | collective-permute-start | bytes 98312 | tf_op jit(solution)/shard_map/ppermute | solution.py:15
  128.5 5.2 %collective-permute-start.17 = (bf16[8,1,4,512]{3,2,1,0:T(4,128)(2,1)S(1)}, bf16[8,1,4,512]{3,2,1,0:T(4,128)(2,1)S(1)}, u32[]{:S(2)}, u32[]{:S(2)}) collective-permute-start(bf16[8,1,4,512]{3,2,1,0:T(4,128)(2,1)S(1)} %get-tuple-element.153), channel_id=1, source_target_pairs={{2,0},{4,2},{6,4},{3,1},{5,3},{7,5},{10,8},{12,10},{14,12},{11,9},... | collective-permute-start | bytes 98312 | tf_op jit(solution)/shard_map/ppermute | solution.py:17
  134.1 4.4 %collective-permute-start.18 = (bf16[8,6,1,512]{3,2,1,0:T(2,128)(2,1)S(1)}, bf16[8,6,1,512]{3,2,1,0:T(2,128)(2,1)S(1)}, u32[]{:S(2)}, u32[]{:S(2)}) collective-permute-start(bf16[8,6,1,512]{3,2,1,0:T(2,128)(2,1)S(1)} %get-tuple-element.142), channel_id=1, source_target_pairs={{0,1},{2,3},{4,5},{6,7},{8,9},{10,11},{12,13},{14,15},{16,17},{18,... | collective-permute-start | bytes 147464 | tf_op jit(solution)/shard_map/ppermute | solution.py:15
  135.4 5.4 %collective-permute-start.19 = (bf16[8,6,1,512]{3,2,1,0:T(2,128)(2,1)S(1)}, bf16[8,6,1,512]{3,2,1,0:T(2,128)(2,1)S(1)}, u32[]{:S(2)}, u32[]{:S(2)}) collective-permute-start(bf16[8,6,1,512]{3,2,1,0:T(2,128)(2,1)S(1)} %get-tuple-element.143), channel_id=1, source_target_pairs={{1,0},{3,2},{5,4},{7,6},{9,8},{11,10},{13,12},{15,14},{17,16},{19,... | collective-permute-start | bytes 147464 | tf_op jit(solution)/shard_map/ppermute | solution.py:17
  154.0 9.9 %copy-start.7 = (f32[128,128]{1,0:T(8,128)S(1)}, f32[128,128]{1,0:T(8,128)}, u32[]{:S(2)}) copy-start(f32[128,128]{1,0:T(8,128)} %fusion.157) | copy-start | bytes 196612
  158.4 9.8 %copy-start.6 = (f32[128,128]{1,0:T(8,128)S(1)}, f32[128,128]{1,0:T(8,128)}, u32[]{:S(2)}) copy-start(f32[128,128]{1,0:T(8,128)} %fusion.151) | copy-start | bytes 196612
  185.4 5.0 %collective-permute-start.20 = (bf16[1,8,8,768]{3,2,1,0:T(8,128)(2,1)S(1)}, bf16[1,8,8,768]{3,2,1,0:T(8,128)(2,1)S(1)}, u32[]{:S(2)}, u32[]{:S(2)}) collective-permute-start(bf16[1,8,8,768]{3,2,1,0:T(8,128)(2,1)S(1)} %get-tuple-element.95), channel_id=1, source_target_pairs={{0,8},{8,16},{16,24},{1,9},{9,17},{17,25},{2,10},{10,18},{18,26},{... | collective-permute-start | bytes 294920 | tf_op jit(solution)/shard_map/ppermute | solution.py:15
  187.8 5.4 %collective-permute-start.21 = (bf16[1,8,8,768]{3,2,1,0:T(8,128)(2,1)S(1)}, bf16[1,8,8,768]{3,2,1,0:T(8,128)(2,1)S(1)}, u32[]{:S(2)}, u32[]{:S(2)}) collective-permute-start(bf16[1,8,8,768]{3,2,1,0:T(8,128)(2,1)S(1)} %get-tuple-element.96), channel_id=1, source_target_pairs={{8,0},{16,8},{24,16},{9,1},{17,9},{25,17},{10,2},{18,10},{26,18},{... | collective-permute-start | bytes 294920 | tf_op jit(solution)/shard_map/ppermute | solution.py:17
  194.5 9.0 %collective-permute-start.22 = (bf16[6,1,8,768]{3,2,1,0:T(8,128)(2,1)S(1)}, bf16[6,1,8,768]{3,2,1,0:T(8,128)(2,1)S(1)}, u32[]{:S(2)}, u32[]{:S(2)}) collective-permute-start(bf16[6,1,8,768]{3,2,1,0:T(8,128)(2,1)S(1)} %get-tuple-element.68), channel_id=1, source_target_pairs={{0,2},{2,4},{4,6},{1,3},{3,5},{5,7},{8,10},{10,12},{12,14},{9,11},... | collective-permute-start | bytes 221192 | tf_op jit(solution)/shard_map/ppermute | solution.py:15
  200.4 5.7 %collective-permute-start.23 = (bf16[6,1,8,768]{3,2,1,0:T(8,128)(2,1)S(1)}, bf16[6,1,8,768]{3,2,1,0:T(8,128)(2,1)S(1)}, u32[]{:S(2)}, u32[]{:S(2)}) collective-permute-start(bf16[6,1,8,768]{3,2,1,0:T(8,128)(2,1)S(1)} %get-tuple-element.69), channel_id=1, source_target_pairs={{2,0},{4,2},{6,4},{3,1},{5,3},{7,5},{10,8},{12,10},{14,12},{11,9},... | collective-permute-start | bytes 221192 | tf_op jit(solution)/shard_map/ppermute | solution.py:17
  206.3 11.3 %collective-permute-start.24 = (bf16[6,10,1,768]{3,2,1,0:T(2,128)(2,1)S(1)}, bf16[6,10,1,768]{3,2,1,0:T(2,128)(2,1)S(1)}, u32[]{:S(2)}, u32[]{:S(2)}) collective-permute-start(bf16[6,10,1,768]{3,2,1,0:T(2,128)(2,1)S(1)} %get-tuple-element.44), channel_id=1, source_target_pairs={{0,1},{2,3},{4,5},{6,7},{8,9},{10,11},{12,13},{14,15},{16,17},{18,... | collective-permute-start | bytes 276488 | tf_op jit(solution)/shard_map/ppermute | solution.py:15
  207.8 9.8 %collective-permute-start.25 = (bf16[6,10,1,768]{3,2,1,0:T(2,128)(2,1)S(1)}, bf16[6,10,1,768]{3,2,1,0:T(2,128)(2,1)S(1)}, u32[]{:S(2)}, u32[]{:S(2)}) collective-permute-start(bf16[6,10,1,768]{3,2,1,0:T(2,128)(2,1)S(1)} %get-tuple-element.43), channel_id=1, source_target_pairs={{1,0},{3,2},{5,4},{7,6},{9,8},{11,10},{13,12},{15,14},{17,16},{19,... | collective-permute-start | bytes 276488 | tf_op jit(solution)/shard_map/ppermute | solution.py:17
  209.4 9.9 %slice-start = ((s8[10616832]{0:T(1024)(128)(4,1)}), s8[4194304]{0:T(1024)(128)(4,1)S(1)}, s32[]{:S(2)}) async-start(s8[10616832]{0:T(1024)(128)(4,1)} %bitcast.627), calls=%async_computation.1 | async-start | bytes 8388608
  212.3 7.0 %slice-start.1 = ((s8[10616832]{0:T(1024)(128)(4,1)}), s8[4194304]{0:T(1024)(128)(4,1)S(1)}, s32[]{:S(2)}) async-start(s8[10616832]{0:T(1024)(128)(4,1)} %bitcast.627), calls=%async_computation.2 | async-start | bytes 8388608
  (8 other events, 19.4 us)
where the time goes:
time: 228 us; the launch traced here: 226 us
  matrix products  69.5 us (30%)
  starting transfers between devices  64.5 us (28%)
  waiting for transfers between devices  36.7 us (16%)
  blocking collectives  26.5 us (12%)
  local copies, waits for them, and re-layouts  15.9 us (7%)
  other arithmetic  10.6 us (5%)
    dot_general x135, matrix products, convolve(): jnp.dot(window.reshape(-1, channels), kernel[offset_x, offset_y, offset_z...  69.5 us
    ppermute x13, starting transfers between devices, with_halo(): lax.ppermute(tail, axis, [(i, (i + 1) % count) for i in range(ends)])  44 us
    ppermute x13, waiting for transfers between devices, with_halo(): lax.ppermute(head, axis, [((i + 1) % count, i) for i in range(ends)])  36.7 us
    ppermute x13, starting transfers between devices, with_halo(): lax.ppermute(head, axis, [((i + 1) % count, i) for i in range(ends)])  20.5 us
    all_gather x1, blocking collectives, on_device(): column = lax.all_gather(coarse, 'gx', axis=0, tiled=True)  10.6 us
    concatenate x16, other arithmetic, with_halo(): jnp.concatenate([lax.ppermute(tail, axis, [(i, (i + 1) % count) for i in...  9.53 us
    all_gather x1, blocking collectives, on_device(): filters = lax.all_gather(bottom_first, 'gx', axis=3, tiled=True)  9 us
    reshape x54, local copies, waits for them, and re-layouts, convolve(): window.reshape(-1, channels)  7.16 us
  transfers between devices with their start and end apart: 26, of which 12 were waited for; matrix products, arithmetic and copies ran while one was open for 6% of the time, Pallas kernels for 0%

commit v1 on v0

v1 whole, which is shorter than its diff:
```python
import functools

import jax
import jax.numpy as jnp
from jax import lax
from jax.experimental import pallas as pl
from jax.experimental.pallas import tpu as pltpu
from jax.sharding import PartitionSpec as P

F32 = jnp.float32
BF16 = jnp.bfloat16
STEPS = [(dx, dy) for dx in (-1, 0, 1) for dy in (-1, 0, 1)]


def span(d, n, pad):
    if d == 0:
        return pl.ds(pad, n), pl.ds(1, n)
    if d < 0:
        return pl.ds(pad, 1), pl.ds(n + 1, 1)
    return pl.ds(pad + n - 1, 1), pl.ds(0, 1)


def kernel(
    dims,
    v, wf_h, wh_h, w1_h, w2_h, wu_h,
    out,
    wf, wh, w1, w2, wu, wsem,
    p1, f1, g1, e1, t1,
    p2, f2, g2, e2,
    p3, f3, g3, e3, acc,
    pk2, l2, sel2, q2, pk3, l3, q3, pk4, l4, vup,
    s1, r1, s2, r2, s3, r3, s4, r4, s5, r5, s6, r6,
):
    gxn, gyn = dims
    gx, gy, gz = lax.axis_index("gx"), lax.axis_index("gy"), lax.axis_index("gz")
    oz = 1 - gz

    loads = [
        pltpu.make_async_copy(src, dst, wsem.at[i])
        for i, (src, dst) in enumerate(((wf_h, wf), (wh_h, wh), (w1_h, w1), (w2_h, w2), (wu_h, wu)))
    ]
    for load in loads:
        load.start()

    def on(cond, fn):
        if cond is True:
            fn()
        else:
            pl.when(cond)(fn)

    def exists(dx, dy):
        conds = []
        if dx < 0:
            conds.append(gx > 0)
        if dx > 0:
            conds.append(gx < gxn - 1)
        if dy < 0:
            conds.append(gy > 0)
        if dy > 0:
            conds.append(gy < gyn - 1)
        if not conds:
            return True
        return functools.reduce(jnp.logical_and, conds)

    for ref in (p1, g1, p2, g2, p3, g3, l2, l3, l4):
        ref[...] = jnp.zeros(ref.shape, ref.dtype)

    barrier = pltpu.get_barrier_semaphore()
    for s in range(gxn):
        there = lax.rem(gx + s, gxn)
        for dy in (-1, 0, 1):
            for z in (0, 1):
                if s == 0 and dy == 0 and z == 0:
                    continue

                def signal(there=there, dy=dy, z=z):
                    pl.semaphore_signal(
                        barrier, inc=1,
                        device_id={"gx": there, "gy": gy + dy, "gz": oz if z else gz},
                        device_id_type=pl.DeviceIdType.MESH,
                    )

                on(exists(0, dy), signal)
    lines = 1 + (gy > 0).astype(jnp.int32) + (gy < gyn - 1).astype(jnp.int32)
    pl.semaphore_wait(barrier, 2 * gxn * lines - 1)

    def send(src, dst, ss, rs, x, y, z):
        return pltpu.make_async_remote_copy(
            src_ref=src, dst_ref=dst, send_sem=ss, recv_sem=rs,
            device_id={"gx": x, "gy": y, "gz": z}, device_id_type=pl.DeviceIdType.MESH,
        )

    late = []

    def neighbours(src, pad, face, rim, side, nx, ny, ss, rs):
        arrivals = []
        for i, (dx, dy) in enumerate(STEPS):
            sx, tx = span(dx, nx, pad)
            sy, ty = span(dy, ny, pad)
            fx, _ = span(dx, nx, 0)
            fy, _ = span(dy, ny, 0)
            copies = [send(face.at[fx, fy], side.at[tx, ty], ss.at[9 + i], rs.at[9 + i], gx + dx, gy + dy, oz)]
            if (dx, dy) != (0, 0):
                copies.append(send(src.at[sx, sy], rim.at[tx, ty], ss.at[i], rs.at[i], gx + dx, gy + dy, gz))
            for copy in copies:
                on(exists(dx, dy), copy.start)
                late.append((exists(dx, dy), copy.wait_send))
                arrivals.append((exists(-dx, -dy), copy.wait_recv))

        def wait():
            for cond, fn in arrivals:
                on(cond, fn)

        return wait

    def edge(block):
        size = block.shape[-2]
        rows = lax.broadcasted_iota(jnp.int32, block.shape, block.ndim - 2)
        return jnp.sum(jnp.where(rows == (size - 1) * oz, block, 0.0), axis=block.ndim - 2, keepdims=True)

    def shifted(block, fill):
        size = block.shape[-2]
        axis = block.ndim - 2
        rows = lax.broadcasted_iota(jnp.int32, block.shape, axis)
        below = jnp.where(rows == 0, 0.0, pltpu.roll(block, 1, axis))
        above = jnp.where(rows == size - 1, 0.0, pltpu.roll(block, size - 1, axis))
        if fill is not None:
            fill = jnp.broadcast_to(fill, block.shape)
            below = jnp.where(rows == jnp.where(gz == 1, 0, -1), fill, below)
            above = jnp.where(rows == jnp.where(gz == 0, size - 1, -1), fill, above)
        return below, above

    def rounded(x):
        return x.astype(BF16).astype(F32)

    nx, ny, nz, c0 = v.shape
    for x in range(nx):
        f1[x] = edge(v[x].astype(F32))
    arrived = neighbours(v, 0, f1, p1, g1, nx, ny, s1, r1)
    p1[1 : nx + 1, 1 : ny + 1] = v[...]
    arrived()

    @pl.loop(0, nx + 2)
    def _(x):
        block = p1[x].astype(F32)
        below, above = shifted(block, g1[x])
        e1[x, :, :, 0:c0] = below.astype(BF16)
        e1[x, :, :, c0 : 2 * c0] = p1[x]
        e1[x, :, :, 2 * c0 :] = above.astype(BF16)

    loads[0].wait()

    def full_row(x):
        total = jnp.zeros((ny * nz, c0), F32)
        for ox in range(3):
            for oy in range(3):
                lhs = e1[x + ox, oy : oy + ny].reshape(ny * nz, 3 * c0)
                total = total + jnp.dot(lhs, wf[ox * 3 + oy], preferred_element_type=F32)
        return jnp.maximum(total, 0.0)

    hx, hy, hz = nx // 2, ny // 2, nz // 2

    @pl.loop(0, hx)
    def _(x):
        both = jnp.maximum(full_row(2 * x), full_row(2 * x + 1)).reshape(hy, 2, nz, c0)
        t1[...] = jnp.max(both, axis=1)
        small = jnp.maximum(t1[:, pl.ds(0, hz, stride=2), :], t1[:, pl.ds(1, hz, stride=2), :])
        small = rounded(small)
        p2[x + 1, 1 : hy + 1] = small
        f2[x] = edge(small)

    arrived = neighbours(p2, 1, f2, p2, g2, hx, hy, s2, r2)
    arrived()
    for x in range(hx + 2):
        block = p2[x]
        below, above = shifted(block, g2[x])
        e2[0, x], e2[1, x], e2[2, x] = below, block, above
    loads[1].wait()
    rows = hx * hy * hz
    c1 = wh.shape[2]
    total = jnp.zeros((rows, c1), F32)
    for ox in range(3):
        for oy in range(3):
            for k in range(3):
                lhs = e2[k, ox : ox + hx, oy : oy + hy].reshape(rows, c0).astype(BF16)
                total = total + jnp.dot(lhs, wh[(ox * 3 + oy) * 3 + k], preferred_element_type=F32)
    skip = rounded(jnp.maximum(total, 0.0)).reshape(hx, hy, hz, c1)
    p3[1 : hx + 1, 1 : hy + 1] = skip
    f3[...] = edge(skip)

    cx, cy, cz = hx // 2, hy // 2, hz // 2
    ax = gxn * cx
    group = cz * cx
    m = jnp.max(skip.reshape(cx, 2, cy, 2, hz, c1), axis=(1, 3))
    m = m.reshape(cx * cy * hz, c1)
    m = jnp.maximum(m, pltpu.roll(m, m.shape[0] - 1, 0)).astype(BF16)

    blocks = []
    lane = lax.broadcasted_iota(jnp.int32, (group, cx * cy * hz), 1)
    sub = lax.broadcasted_iota(jnp.int32, (group, cx * cy * hz), 0)
    shift_x = cx.bit_length() - 1
    sub_x = sub & (cx - 1)
    sub_o = sub >> shift_x
    for y in range(cy):
        blocks.append(jnp.where(lane == (sub_x * cy + y) * hz + 2 * sub_o, 1.0, 0.0))
    blocks.append(jnp.where(lane == (sub_x * cy + sub_o) * hz + 2 * (cz - 1) * oz, 1.0, 0.0))
    pick = jnp.concatenate(blocks, axis=0).astype(BF16)
    packets = jnp.dot(pick, m, preferred_element_type=F32).reshape(cy + 1, group, c1).astype(BF16)
    pk2[...] = packets
    l2[gx, 0:cy] = packets[0:cy]

    slots = cy + 5

    def coarse_copy(s, dy, z, k):
        def make(src_gx, tgt_gx):
            if z == 0:
                src = {0: pl.ds(0, cy), -1: pl.ds(0, 1), 1: pl.ds(cy - 1, 1)}[dy]
                dst = {0: pl.ds(0, cy), 1: pl.ds(cy, 1), -1: pl.ds(cy + 1, 1)}[dy]
            else:
                src = pl.ds(cy, 1)
                dst = {0: pl.ds(cy + 2, 1), 1: pl.ds(cy + 3, 1), -1: pl.ds(cy + 4, 1)}[dy]
            return send(pk2.at[src], l2.at[src_gx, dst], s4.at[s, k], r4.at[s, k], tgt_gx, gy + dy, oz if z else gz)

        return make

    def deep_copy(pk, land, ss, rs):
        def choose(s, dy, z, k):
            def make(src_gx, tgt_gx):
                sy, ty = span(dy, cy, 0)
                sender = gz if src_gx is gx else (oz if z else gz)
                if z == 0:
                    src = pk.at[sy]
                    dst = land.at[src_gx, ty, pl.ds(1, cz)]
                else:
                    src = pk.at[sy, pl.ds((cz - 1) * (1 - sender), 1)]
                    dst = land.at[src_gx, ty, pl.ds((cz + 1) * sender, 1)]
                return send(src, dst, ss.at[s, k], rs.at[s, k], tgt_gx, gy + dy, oz if z else gz)

            return make

        return choose

    def column_exchange(choose):
        arrivals = []
        for s in list(range(1, gxn)) + [0]:
            there = lax.rem(gx + s, gxn)
            origin = lax.rem(gx + gxn - s, gxn)
            for k, (dy, z) in enumerate(((0, 0), (-1, 0), (1, 0), (0, 1), (-1, 1), (1, 1))):
                if s == 0 and k == 0:
                    continue
                make = choose(s, dy, z, k)
                copy = make(gx, there)
                on(exists(0, dy), copy.start)
                late.append((exists(0, dy), copy.wait_send))
                arrivals.append((exists(0, -dy), make(origin, there).wait_recv))

        def wait():
            for cond, fn in arrivals:
                on(cond, fn)

        return wait

    arrived = column_exchange(coarse_copy)
    skip_arrived = neighbours(p3, 1, f3, p3, g3, hx, hy, s3, r3)

    span_g = slots * group
    width = gxn * span_g
    lane = lax.broadcasted_iota(jnp.int32, (ax, width), 1)
    xs = lax.broadcasted_iota(jnp.int32, (ax, width), 0)
    base = lane - ((xs >> shift_x) * span_g + (xs & (cx - 1)))
    for y in range(-1, cy + 1):
        for z in range(-1, cz + 1):
            if 0 <= z < cz:
                slot = y if 0 <= y < cy else (cy if y < 0 else cy + 1)
                at = slot * group + z * cx
            else:
                slot = cy + 2 if 0 <= y < cy else (cy + 3 if y < 0 else cy + 4)
                line = y if 0 <= y < cy else (cy - 1 if y < 0 else 0)
                mine = (gz == 1) if z < 0 else (gz == 0)
                at = jnp.where(mine, slot * group + line * cx, -width * 4)
            sel2[y + 1, z + 1] = jnp.where(base == at, 1.0, 0.0)

    rim = (cy + 2) * (cz + 2) * ax
    select = sel2[...].reshape(rim, width).astype(BF16)
    arrived()
    landed = l2[...].astype(F32).reshape(width, c1).astype(BF16)
    block = jnp.dot(select, landed, preferred_element_type=F32).reshape(cy + 2, cz + 2, ax, c1)

    def spread(q, block):
        below, above = shifted(block, None)
        q[0], q[1], q[2] = below, block, above

    deep = cy * cz * ax
    fo = w1.shape[2]

    def bottom(q, w):
        total = jnp.zeros((deep, fo), F32)
        for ox in range(3):
            for oy in range(3):
                for k in range(3):
                    lhs = q[ox, oy : oy + cy, k : k + cz].reshape(deep, q.shape[-1]).astype(BF16)
                    total = total + jnp.dot(lhs, w[(ox * 3 + oy) * 3 + k], preferred_element_type=F32)
        return jnp.maximum(total, 0.0).reshape(cy, cz, ax, fo).astype(BF16)

    spread(q2, block)
    loads[2].wait()
    first = bottom(q2, w1)
    pk3[...] = first
    l3[gx, 1 : cy + 1, 1 : cz + 1] = first
    arrived = column_exchange(deep_copy(pk3, l3, s5, r5))

    skip_arrived()
    for x in range(hx + 2):
        block = p3[x]
        below, above = shifted(block, g3[x])
        e3[0, x], e3[1, x], e3[2, x] = below, block, above
    loads[4].wait()
    c2 = w2.shape[1]
    total = jnp.zeros((rows, c1), F32)
    for ox in range(3):
        for oy in range(3):
            for k in range(3):
                lhs = e3[k, ox : ox + hx, oy : oy + hy].reshape(rows, c1).astype(BF16)
                total = total + jnp.dot(lhs, wu[(ox * 3 + oy) * 3 + k, c2:, :], preferred_element_type=F32)
    acc[...] = total.reshape(hx, hy, hz, c1)

    arrived()
    spread(q3, jnp.concatenate([l3[g].astype(F32) for g in range(gxn)], axis=-1))
    loads[3].wait()
    second = bottom(q3, w2)
    pk4[...] = second
    l4[gx, 1 : cy + 1, 1 : cz + 1] = second
    arrived = column_exchange(deep_copy(pk4, l4, s6, r6))

    lane = lax.broadcasted_iota(jnp.int32, (hz, (cz + 2) * ax), 1)
    zs = lax.broadcasted_iota(jnp.int32, (hz, (cz + 2) * ax), 0)
    blocks = []
    for k in range(3):
        for x in range(-1, hx + 1):
            at = gx * cx + (x >> 1)
            at = jnp.where(jnp.logical_and(at >= 0, at < ax), at, -(cz + 3) * ax)
            blocks.append(jnp.where(lane == ((zs + (k + 1)) >> 1) * ax + at, 1.0, 0.0))
    pick = jnp.concatenate(blocks, axis=0).astype(BF16)

    arrived()
    for y in range(cy + 2):
        field = jnp.concatenate([l4[g, y].astype(F32) for g in range(gxn)], axis=-1)
        field = field.reshape((cz + 2) * ax, c2).astype(BF16)
        vup[:, y] = jnp.dot(pick, field, preferred_element_type=F32).reshape(3, hx + 2, hz, c2)

    parts = []
    for oy in range(3):
        low, high = (oy + 1) // 2, (hy - 1 + oy + 1) // 2 + 1
        count = high - low
        total = jnp.zeros((count * hx * hz, c1), F32)
        for ox in range(3):
            for k in range(3):
                lhs = vup[k, low:high, ox : ox + hx].reshape(count * hx * hz, c2).astype(BF16)
                total = total + jnp.dot(lhs, wu[(ox * 3 + oy) * 3 + k, :c2, :], preferred_element_type=F32)
        parts.append((low, total.reshape(count, hx, hz, c1)))
    for y in range(hy):
        line = acc[:, y]
        for oy in range(3):
            low, part = parts[oy]
            line = line + part[(y + oy + 1) // 2 - low]
        out[:, y] = line.astype(BF16)

    for cond, fn in late:
        on(cond, fn)


def on_device(dims, volume, w_full, w_half, w_bottom_in, w_bottom_out, w_up):
    gxn, gyn = dims
    nx, ny, nz, c0 = volume.shape
    c1 = w_half.shape[4]
    c2, fo = w_bottom_out.shape[3:]
    hx, hy, hz = nx // 2, ny // 2, nz // 2
    cx, cy, cz = hx // 2, hy // 2, hz // 2
    ax = gxn * cx
    weights = [
        w_full.reshape(9, 3 * c0, c0),
        w_half.reshape(27, c0, c1),
        w_bottom_in.reshape(27, c1, fo),
        w_bottom_out.reshape(27, c2, fo),
        w_up.reshape(27, c2 + c1, c1),
    ]
    vm = pltpu.VMEM
    dma = pltpu.SemaphoreType.DMA
    scratch = [vm(w.shape, BF16) for w in weights] + [dma((5,))]
    scratch += [
        vm((nx + 2, ny + 2, nz, c0), BF16), vm((nx, ny, 1, c0), F32), vm((nx + 2, ny + 2, 1, c0), F32),
        vm((nx + 2, ny + 2, nz, 3 * c0), BF16), vm((hy, nz, c0), F32),
        vm((hx + 2, hy + 2, hz, c0), F32), vm((hx, hy, 1, c0), F32), vm((hx + 2, hy + 2, 1, c0), F32),
        vm((3, hx + 2, hy + 2, hz, c0), F32),
        vm((hx + 2, hy + 2, hz, c1), F32), vm((hx, hy, 1, c1), F32), vm((hx + 2, hy + 2, 1, c1), F32),
        vm((3, hx + 2, hy + 2, hz, c1), F32), vm((hx, hy, hz, c1), F32),
        vm((cy + 1, cz * cx, c1), BF16), vm((gxn, cy + 5, cz * cx, c1), BF16),
        vm((cy + 2, cz + 2, ax, gxn * (cy + 5) * cz * cx), F32), vm((3, cy + 2, cz + 2, ax, c1), F32),
        vm((cy, cz, ax, fo), BF16), vm((gxn, cy + 2, cz + 2, ax, fo), BF16), vm((3, cy + 2, cz + 2, ax, c2), F32),
        vm((cy, cz, ax, fo), BF16), vm((gxn, cy + 2, cz + 2, ax, fo), BF16),
        vm((3, cy + 2, hx + 2, hz, c2), F32),
    ]
    scratch += [dma((18,))] * 6 + [dma((gxn, 6))] * 6
    return pl.pallas_call(
        functools.partial(kernel, dims),
        out_shape=jax.ShapeDtypeStruct((hx, hy, hz, c1), BF16),
        in_specs=[pl.BlockSpec(memory_space=pltpu.VMEM)] + [pl.BlockSpec(memory_space=pl.ANY)] * 5,
        out_specs=pl.BlockSpec(memory_space=pltpu.VMEM),
        scratch_shapes=scratch,
        compiler_params=pltpu.CompilerParams(
            collective_id=0, has_side_effects=True, vmem_limit_bytes=60 * 1024 * 1024
        ),
    )(volume, *weights)


def solution(mesh):
    dims = (mesh.shape["gx"], mesh.shape["gy"])
    assert mesh.shape["gz"] == 2
    return jax.shard_map(
        functools.partial(on_device, dims),
        mesh=mesh,
        in_specs=(
            P("gx", "gy", "gz", None),
            P(),
            P(),
            P(None, None, None, None, "gx"),
            P(None, None, None, None, "gx"),
            P(),
        ),
        out_specs=P("gx", "gy", "gz", None),
        check_vma=False,
    )
```

time: 228 us -> 51.4 us (0.23)
  matrix products: 69.5 us -> 0 us
  starting transfers between devices: 64.5 us -> 0 us
  Pallas kernels: 0 us -> 49.6 us
  waiting for transfers between devices: 36.7 us -> 0 us
  blocking collectives: 26.5 us -> 0 us
  local copies, waits for them, and re-layouts: 15.9 us -> 1.57 us
  other arithmetic: 10.6 us -> 0 us
    dot_general x135 -> x0, matrix products: 69.5 us -> none  [convolve(): jnp.dot(window.reshape(-1, channels), kernel[offset_x, offset_y, offset_z...]
    ppermute x26 -> x0, starting transfers between devices: 64.5 us -> none  [the longest x13 44 us: with_halo(): lax.ppermute(tail, axis, [(i, (i + 1) % count) for i in range(ends)])]
    pallas_call x0 -> x1, Pallas kernels: none -> 49.6 us  [on_device(): pl.pallas_call(functools.partial(kernel, dims), out_shape=jax.ShapeDtypeS...]
    ppermute x26 -> x0, waiting for transfers between devices: 36.7 us -> none  [the longest x13 36.7 us: with_halo(): lax.ppermute(head, axis, [((i + 1) % count, i) for i in range(ends)])]
    all_gather x2 -> x0, blocking collectives: 19.6 us -> none  [the longest x1 10.6 us: on_device(): column = lax.all_gather(coarse, 'gx', axis=0, tiled=True)]
    concatenate x16 -> x0, other arithmetic: 9.53 us -> none  [with_halo(): jnp.concatenate([lax.ppermute(tail, axis, [(i, (i + 1) % count) for i in...]
    reshape x55 -> x0, local copies, waits for them, and re-layouts: 7.26 us -> none  [the longest x54 7.16 us: convolve(): window.reshape(-1, channels)]
    all_to_all x1 -> x0, blocking collectives: 6.93 us -> none  [on_device(): lax.all_to_all(bottom_second, 'gx', split_axis=0, concat_axis=3, tiled=True)]
  transfers between devices with their start and end apart: 26 -> 0, of which waited for: 12 -> 0; matrix products, arithmetic and copies ran while one was open for 6% -> 0% of each run, Pallas kernels for 0% -> 0%
where the time goes in v1:
time: 51.4 us; the launch traced here: 51.2 us
  Pallas kernels  49.6 us (96%)
  local copies, waits for them, and re-layouts  1.57 us (3%)
    pallas_call x1, Pallas kernels, on_device(): pl.pallas_call(functools.partial(kernel, dims), out_shape=jax.ShapeDtypeS...  49.6 us
    unnamed x1, local copies, waits for them, and re-layouts  1.57 us

profile of v1, /device:TPU:1, one launch (start us, length us, event | category | flops | bytes accessed | tf_op | source)
XLA Modules:
  0.0 51.2 jit_solution(6090922804206256889)
XLA Ops:
  0.0 49.6 %shard_map.64 = bf16[4,8,8,256]{3,2,1,0:T(8,128)(2,1)} custom-call(bf16[8,16,16,128]{3,2,1,0:T(8,128)(2,1)} %v.1, bf16[9,384,128]{2,1,0:T(8,128)(2,1)} %bitcast.9, bf16[27,128,256]{2,1,0:T(8,128)(2,1)} %bitcast.7, bf16[27,256,128]{2,1,0:T(8,128)(2,1)} %bitcast.8, bf16[27,512,128]{2,1,0:T(8,128)(2,1)} %bitcast.6, bf16[27,768,256]{2,1,0:T(8,128)(2,1)} %bitcast.5), custom_call_target="tpu_custom_call" | custom-call | tf_op jit(solution)/shard_map/pallas_call | solution.py:404
  49.6 1.6 %copy.8 = bf16[4,8,8,256]{3,2,1,0:T(8,128)(2,1)} copy(bf16[4,8,8,256]{3,2,1,0:T(8,128)(2,1)} %shard_map.64) | data formatting | bytes 262144

commit v2 on v1

--- a/solution.py
+++ b/solution.py
@@ -240,6 +240,20 @@
 
         return choose
 
+    def narrow_copy(s, dy, z, k):
+        def make(src_gx, tgt_gx):
+            sy, ty = span(dy, cy, 0)
+            sender = gz if src_gx is gx else (oz if z else gz)
+            if z == 0:
+                src = pk4.at[tgt_gx, sy]
+                dst = l4.at[src_gx, ty, pl.ds(1, cz // 2)]
+            else:
+                src = pk4.at[tgt_gx, sy, pl.ds((cz // 2 - 1) * (1 - sender), 1)]
+                dst = l4.at[src_gx, ty, pl.ds((cz // 2 + 1) * sender, 1)]
+            return send(src, dst, s6.at[s, k], r6.at[s, k], tgt_gx, gy + dy, oz if z else gz)
+
+        return make
+
     def column_exchange(choose):
         arrivals = []
         for s in list(range(1, gxn)) + [0]:
@@ -261,7 +275,6 @@
         return wait
 
     arrived = column_exchange(coarse_copy)
-    skip_arrived = neighbours(p3, 1, f3, p3, g3, hx, hy, s3, r3)
 
     span_g = slots * group
     width = gxn * span_g
@@ -283,6 +296,7 @@
     rim = (cy + 2) * (cz + 2) * ax
     select = sel2[...].reshape(rim, width).astype(BF16)
     arrived()
+    skip_arrived = neighbours(p3, 1, f3, p3, g3, hx, hy, s3, r3)
     landed = l2[...].astype(F32).reshape(width, c1).astype(BF16)
     block = jnp.dot(select, landed, preferred_element_type=F32).reshape(cy + 2, cz + 2, ax, c1)
 
@@ -324,28 +338,38 @@
                 total = total + jnp.dot(lhs, wu[(ox * 3 + oy) * 3 + k, c2:, :], preferred_element_type=F32)
     acc[...] = total.reshape(hx, hy, hz, c1)
 
+    near = cx + 2
+    wide = gxn * cz * near
+    lane = lax.broadcasted_iota(jnp.int32, (wide, cz * ax), 1)
+    row = lax.broadcasted_iota(jnp.int32, (wide, cz * ax), 0)
+    shift_n = near.bit_length() - 1
+    shift_z = cz.bit_length() - 1
+    at = (row >> (shift_n + shift_z)) * cx + (row & (near - 1)) - 1
+    at = jnp.where(jnp.logical_and(at >= 0, at < ax), at, -(cz + 1) * ax)
+    share = jnp.where(lane == ((row >> shift_n) & (cz - 1)) * ax + at, 1.0, 0.0).astype(BF16)
+
+    lane = lax.broadcasted_iota(jnp.int32, (hz, (cz + 4) * near), 1)
+    zs = lax.broadcasted_iota(jnp.int32, (hz, (cz + 4) * near), 0)
+    blocks = []
+    for k in range(3):
+        for x in range(-1, hx + 1):
+            blocks.append(jnp.where(lane == (((zs + (k - 1)) >> 1) + 2) * near + (x >> 1) + 1, 1.0, 0.0))
+    pick = jnp.concatenate(blocks, axis=0).astype(BF16)
+
     arrived()
     spread(q3, jnp.concatenate([l3[g].astype(F32) for g in range(gxn)], axis=-1))
     loads[3].wait()
     second = bottom(q3, w2)
-    pk4[...] = second
-    l4[gx, 1 : cy + 1, 1 : cz + 1] = second
-    arrived = column_exchange(deep_copy(pk4, l4, s6, r6))
-
-    lane = lax.broadcasted_iota(jnp.int32, (hz, (cz + 2) * ax), 1)
-    zs = lax.broadcasted_iota(jnp.int32, (hz, (cz + 2) * ax), 0)
-    blocks = []
-    for k in range(3):
-        for x in range(-1, hx + 1):
-            at = gx * cx + (x >> 1)
-            at = jnp.where(jnp.logical_and(at >= 0, at < ax), at, -(cz + 3) * ax)
-            blocks.append(jnp.where(lane == ((zs + (k + 1)) >> 1) * ax + at, 1.0, 0.0))
-    pick = jnp.concatenate(blocks, axis=0).astype(BF16)
-
+    for y in range(cy):
+        line = second[y].astype(F32).reshape(cz * ax, fo).astype(BF16)
+        line = jnp.dot(share, line, preferred_element_type=F32)
+        pk4[:, y] = line.reshape(gxn, cz // 2, 2 * near, fo).astype(BF16)
+    l4[gx, 1 : cy + 1, 1 : cz // 2 + 1] = pk4[gx]
+    arrived = column_exchange(narrow_copy)
     arrived()
     for y in range(cy + 2):
         field = jnp.concatenate([l4[g, y].astype(F32) for g in range(gxn)], axis=-1)
-        field = field.reshape((cz + 2) * ax, c2).astype(BF16)
+        field = field.reshape((cz + 4) * near, c2).astype(BF16)
         vup[:, y] = jnp.dot(pick, field, preferred_element_type=F32).reshape(3, hx + 2, hz, c2)
 
     parts = []
@@ -397,7 +421,7 @@
         vm((cy + 1, cz * cx, c1), BF16), vm((gxn, cy + 5, cz * cx, c1), BF16),
         vm((cy + 2, cz + 2, ax, gxn * (cy + 5) * cz * cx), F32), vm((3, cy + 2, cz + 2, ax, c1), F32),
         vm((cy, cz, ax, fo), BF16), vm((gxn, cy + 2, cz + 2, ax, fo), BF16), vm((3, cy + 2, cz + 2, ax, c2), F32),
-        vm((cy, cz, ax, fo), BF16), vm((gxn, cy + 2, cz + 2, ax, fo), BF16),
+        vm((gxn, cy, cz // 2, 2 * (cx + 2), fo), BF16), vm((gxn, cy + 2, cz // 2 + 2, 2 * (cx + 2), fo), BF16),
         vm((3, cy + 2, hx + 2, hz, c2), F32),
     ]
     scratch += [dma((18,))] * 6 + [dma((gxn, 6))] * 6

time: 51.4 us -> 50.6 us (0.984)
  Pallas kernels: 49.6 us -> 48.8 us
    pallas_call x1, Pallas kernels: 49.6 us -> 48.8 us  [on_device(): pl.pallas_call(functools.partial(kernel, dims), out_shape=jax.ShapeDtypeS...]
where the time goes in v2:
time: 50.6 us; the launch traced here: 50.4 us
  Pallas kernels  48.8 us (96%)
  local copies, waits for them, and re-layouts  1.57 us (3%)
    pallas_call x1, Pallas kernels, on_device(): pl.pallas_call(functools.partial(kernel, dims), out_shape=jax.ShapeDtypeS...  48.8 us
    unnamed x1, local copies, waits for them, and re-layouts  1.57 us

profile of v2, /device:TPU:1, one launch (start us, length us, event | category | flops | bytes accessed | tf_op | source)
XLA Modules:
  0.0 50.4 jit_solution(5085524462546513636)
XLA Ops:
  0.0 48.8 %shard_map.64 = bf16[4,8,8,256]{3,2,1,0:T(8,128)(2,1)} custom-call(bf16[8,16,16,128]{3,2,1,0:T(8,128)(2,1)} %v.1, bf16[9,384,128]{2,1,0:T(8,128)(2,1)} %bitcast.9, bf16[27,128,256]{2,1,0:T(8,128)(2,1)} %bitcast.7, bf16[27,256,128]{2,1,0:T(8,128)(2,1)} %bitcast.8, bf16[27,512,128]{2,1,0:T(8,128)(2,1)} %bitcast.6, bf16[27,768,256]{2,1,0:T(8,128)(2,1)} %bitcast.5), custom_call_target="tpu_custom_call" | custom-call | tf_op jit(solution)/shard_map/pallas_call | solution.py:428
  48.8 1.6 %copy.8 = bf16[4,8,8,256]{3,2,1,0:T(8,128)(2,1)} copy(bf16[4,8,8,256]{3,2,1,0:T(8,128)(2,1)} %shard_map.64) | data formatting | bytes 262144

commit v3 on v2

--- a/solution.py
+++ b/solution.py
@@ -24,7 +24,7 @@
     dims,
     v, wf_h, wh_h, w1_h, w2_h, wu_h,
     out,
-    wf, wh, w1, w2, wu, wsem,
+    wf, wh, w1, w2, wu, wsem, wt,
     p1, f1, g1, e1, t1,
     p2, f2, g2, e2,
     p3, f3, g3, e3, acc,
@@ -138,6 +138,14 @@
         f1[x] = edge(v[x].astype(F32))
     arrived = neighbours(v, 0, f1, p1, g1, nx, ny, s1, r1)
     p1[1 : nx + 1, 1 : ny + 1] = v[...]
+
+    loads[0].wait()
+    k0 = 3 * c0
+    for oy in range(3):
+        for plane in range(4):
+            at = pl.ds(plane * k0, k0)
+            wt[oy, at, :c0] = wf[plane * 3 + oy] if plane < 3 else jnp.zeros((k0, c0), BF16)
+            wt[oy, at, c0:] = wf[(plane - 1) * 3 + oy] if plane > 0 else jnp.zeros((k0, c0), BF16)
     arrived()
 
     @pl.loop(0, nx + 2)
@@ -148,21 +156,20 @@
         e1[x, :, :, c0 : 2 * c0] = p1[x]
         e1[x, :, :, 2 * c0 :] = above.astype(BF16)
 
-    loads[0].wait()
-
-    def full_row(x):
-        total = jnp.zeros((ny * nz, c0), F32)
-        for ox in range(3):
-            for oy in range(3):
-                lhs = e1[x + ox, oy : oy + ny].reshape(ny * nz, 3 * c0)
-                total = total + jnp.dot(lhs, wf[ox * 3 + oy], preferred_element_type=F32)
-        return jnp.maximum(total, 0.0)
+    def full_rows(x):
+        total = jnp.zeros((ny * nz, 2 * c0), F32)
+        for oy in range(3):
+            for half in range(2):
+                lhs = [e1[x + 2 * half + i, oy : oy + ny].reshape(ny * nz, k0) for i in range(2)]
+                rhs = wt[oy, 2 * half * k0 : 2 * (half + 1) * k0]
+                total = total + jnp.dot(jnp.concatenate(lhs, axis=1), rhs, preferred_element_type=F32)
+        return jnp.maximum(jnp.maximum(total[:, :c0], total[:, c0:]), 0.0)
 
     hx, hy, hz = nx // 2, ny // 2, nz // 2
 
     @pl.loop(0, hx)
     def _(x):
-        both = jnp.maximum(full_row(2 * x), full_row(2 * x + 1)).reshape(hy, 2, nz, c0)
+        both = full_rows(2 * x).reshape(hy, 2, nz, c0)
         t1[...] = jnp.max(both, axis=1)
         small = jnp.maximum(t1[:, pl.ds(0, hz, stride=2), :], t1[:, pl.ds(1, hz, stride=2), :])
         small = rounded(small)
@@ -410,7 +417,7 @@
     ]
     vm = pltpu.VMEM
     dma = pltpu.SemaphoreType.DMA
-    scratch = [vm(w.shape, BF16) for w in weights] + [dma((5,))]
+    scratch = [vm(w.shape, BF16) for w in weights] + [dma((5,)), vm((3, 12 * c0, 2 * c0), BF16)]
     scratch += [
         vm((nx + 2, ny + 2, nz, c0), BF16), vm((nx, ny, 1, c0), F32), vm((nx + 2, ny + 2, 1, c0), F32),
         vm((nx + 2, ny + 2, nz, 3 * c0), BF16), vm((hy, nz, c0), F32),

time: 50.6 us -> 49.4 us (0.976)
  Pallas kernels: 48.8 us -> 47.6 us
    pallas_call x1, Pallas kernels: 48.8 us -> 47.6 us  [on_device(): pl.pallas_call(functools.partial(kernel, dims), out_shape=jax.ShapeDtypeS...]
where the time goes in v3:
time: 49.4 us; the launch traced here: 49.2 us
  Pallas kernels  47.6 us (96%)
  local copies, waits for them, and re-layouts  1.57 us (3%)
    pallas_call x1, Pallas kernels, on_device(): pl.pallas_call(functools.partial(kernel, dims), out_shape=jax.ShapeDtypeS...  47.6 us
    unnamed x1, local copies, waits for them, and re-layouts  1.57 us

profile of v3, /device:TPU:1, one launch (start us, length us, event | category | flops | bytes accessed | tf_op | source)
XLA Modules:
  0.0 49.2 jit_solution(14770528035685618952)
XLA Ops:
  0.0 47.6 %shard_map.64 = bf16[4,8,8,256]{3,2,1,0:T(8,128)(2,1)} custom-call(bf16[8,16,16,128]{3,2,1,0:T(8,128)(2,1)} %v.1, bf16[9,384,128]{2,1,0:T(8,128)(2,1)} %bitcast.9, bf16[27,128,256]{2,1,0:T(8,128)(2,1)} %bitcast.7, bf16[27,256,128]{2,1,0:T(8,128)(2,1)} %bitcast.8, bf16[27,512,128]{2,1,0:T(8,128)(2,1)} %bitcast.6, bf16[27,768,256]{2,1,0:T(8,128)(2,1)} %bitcast.5), custom_call_target="tpu_custom_call" | custom-call | tf_op jit(solution)/shard_map/pallas_call | solution.py:435
  47.6 1.6 %copy.8 = bf16[4,8,8,256]{3,2,1,0:T(8,128)(2,1)} copy(bf16[4,8,8,256]{3,2,1,0:T(8,128)(2,1)} %shard_map.64) | data formatting | bytes 262144
